TPU v7x, 512 devices: a whole 4x8x8 slice. The times are simulated.
512 devices in a mesh: ta: 64 (over y, x, core), gz: 8 (over z).
Axes of the slice: x: 4, y: 8, z: 8, core: 2. Of those that a mesh axis runs over, the one named last changes fastest.
Arguments:
- time_links: float32 [2, 3, 3, 128, 32, 256], P(None, None, None, 'ta', 'gz'), may hold values from -1 to 1, as said below
- space_links: float32 [3, 2, 3, 3, 128, 32, 256], P(None, None, None, None, 'ta', 'gz'), may hold values from -1 to 1, as said below
Outputs:
- gauge: float32 [2, 3, 3, 128, 32, 256], P(None, None, None, 'ta', 'gz')
- links_fixed: float32 [3, 2, 3, 3, 128, 32, 256], P(None, None, None, None, 'ta', 'gz')
- action_profile: float32 [128, 32], P('ta', 'gz')
- action_mean: float32 [], replicated
Inputs may be any that keep to these rules, and one draw needn't show every extreme that they name: `time_links`: every 3 x 3 complex matrix is unitary up to float32 rounding. `space_links`: every 3 x 3 complex matrix is unitary up to float32 rounding.
All inputs are finite; a program needn't handle non-finite values.
Results may differ from a plain program's by a relative error of at most 0.00024.
Values sent between devices are 32-bit elements; how exact they have to be, the bound alone decides.
A program may use at most 64 MiB of HBM per device.

v0:
```python
import jax
import jax.numpy as jnp
from jax import lax
from jax.sharding import Mesh
from jax.sharding import PartitionSpec as P

X = 16
Y = 16
TA = ("ta_0", "ta_1", "ta_2")
TA_GZ = ("ta_0", "ta_1", "ta_2", "gz")


def filled_with(shard, identity):
    return jnp.broadcast_to(jnp.asarray(identity, shard.dtype), shard.shape)


def carried_in(shard, axes, combine, identity):
    before = start = filled_with(shard, identity)
    so_far = shard
    for axis in reversed(axes):
        length, mine = (lax.axis_size(axis), lax.axis_index(axis))
        pieces = lax.all_gather(so_far, axis)
        inside, so_far = (start, start)
        for k in range(length):
            passed = k < mine
            so_far = combine(so_far, pieces[k])
            inside = jnp.where(passed, so_far, inside)
        before = combine(inside, before)
    return before


def from_behind(block, axis, distance):
    devices = range(lax.axis_size(axis))
    route = [((i - distance) % len(devices), i) for i in devices]
    return lax.ppermute(block, axis, route)


def over_axes(shard, axes):
    for axis in axes:
        shard = lax.psum(shard, axis)
    return shard


def complex_product(first_pair, second_pair):
    first_real, first_imag = first_pair
    second_real, second_imag = second_pair
    real_part = jnp.sum(
        first_real[:, :, None] * second_real[None] - first_imag[:, :, None] * second_imag[None],
        axis=1,
    )
    imag_part = jnp.sum(
        first_real[:, :, None] * second_imag[None] + first_imag[:, :, None] * second_real[None],
        axis=1,
    )
    return (real_part, imag_part)


def dagger(matrix_pair):
    return (jnp.swapaxes(matrix_pair[0], 0, 1), -jnp.swapaxes(matrix_pair[1], 0, 1))


def plane_step(matrix_pair, direction):

    def shifted(values):
        leading = values.shape[:-1]
        lattice_grid = values.reshape(leading + (X, Y))
        lattice_grid = jnp.roll(lattice_grid, -1, axis=lattice_grid.ndim - 2 + direction)
        return lattice_grid.reshape(leading + (X * Y,))

    return (shifted(matrix_pair[0]), shifted(matrix_pair[1]))


def upward_z(matrix_pair, upper_layer):
    return (
        jnp.concatenate([matrix_pair[0][..., 1:, :], upper_layer[0]], axis=-2),
        jnp.concatenate([matrix_pair[1][..., 1:, :], upper_layer[1]], axis=-2),
    )


def plaquette_density(link_set, forward_x, forward_y):
    forward_z = [forward_x, forward_y]
    terms = []
    for first_dir, second_dir in ((0, 1), (0, 2), (1, 2)):
        along_first = link_set[first_dir]
        along_second = link_set[second_dir]
        second_moved = plane_step(along_second, first_dir)
        if second_dir < 2:
            first_moved = plane_step(along_first, second_dir)
        else:
            first_moved = forward_z[first_dir]
        loop_matrix = complex_product(
            complex_product(along_first, second_moved),
            complex_product(dagger(first_moved), dagger(along_second)),
        )
        trace_real = loop_matrix[0][0, 0] + loop_matrix[0][1, 1] + loop_matrix[0][2, 2]
        terms.append(1.0 - trace_real / 3.0)
    return terms[0] + terms[1] + terms[2]


def on_device(time_links, space_links):
    local_steps = time_links.shape[3]
    layer_count = time_links.shape[4]
    site_count = time_links.shape[5]
    unit_matrix = jnp.eye(3, dtype=jnp.float32)[:, :, None, None]
    unit_real = jnp.broadcast_to(unit_matrix, (3, 3, layer_count, site_count))
    running = (unit_real, jnp.zeros_like(unit_real))
    prefixes = []
    for step_index in range(local_steps):
        prefixes.append(running)
        running = complex_product(
            running, (time_links[0, :, :, step_index], time_links[1, :, :, step_index])
        )

    def combine(earlier, later):
        return jnp.stack(complex_product((earlier[0], earlier[1]), (later[0], later[1])))

    identity_pair = jnp.stack([unit_real, jnp.zeros_like(unit_real)])
    carried = carried_in(jnp.stack(running), TA, combine, identity_pair)
    carried_pair = (carried[0], carried[1])
    time_slices = [complex_product(carried_pair, prefix_pair) for prefix_pair in prefixes]
    gauge_pair = (
        jnp.stack([piece[0] for piece in time_slices], axis=2),
        jnp.stack([piece[1] for piece in time_slices], axis=2),
    )
    first_layer = jnp.stack([gauge_pair[0][..., 0:1, :], gauge_pair[1][..., 0:1, :]])
    gauge_above = from_behind(first_layer, "gz", -1)
    gauge_next_z = upward_z(gauge_pair, (gauge_above[0], gauge_above[1]))
    fixed = []
    for direction in range(3):
        link_pair = (space_links[direction, 0], space_links[direction, 1])
        ahead = plane_step(gauge_pair, direction) if direction < 2 else gauge_next_z
        fixed.append(complex_product(complex_product(gauge_pair, link_pair), dagger(ahead)))
    links_fixed = jnp.stack([jnp.stack(pair) for pair in fixed])
    top_layers = jnp.stack(
        [jnp.stack([pair[0][..., 0:1, :], pair[1][..., 0:1, :]]) for pair in fixed[:2]]
    )
    layers_above = from_behind(top_layers, "gz", -1)
    forward_x = upward_z(fixed[0], (layers_above[0, 0], layers_above[0, 1]))
    forward_y = upward_z(fixed[1], (layers_above[1, 0], layers_above[1, 1]))
    density = plaquette_density(fixed, forward_x, forward_y)
    action_profile = jnp.mean(density, axis=-1) / 3.0
    local_total = jnp.sum(action_profile)
    whole_total = over_axes(local_total, TA_GZ)
    action_mean = whole_total / (action_profile.size * lax.axis_size(TA) * lax.axis_size("gz"))
    return (jnp.stack(gauge_pair), links_fixed, action_profile, action_mean)


def solution(mesh):
    finer = Mesh(mesh.devices.reshape(8, 4, 2, mesh.shape["gz"]), ("ta_0", "ta_1", "ta_2", "gz"))
    placed = (P(None, None, None, TA, "gz", None), P(None, None, None, None, TA, "gz", None))
    return jax.shard_map(
        on_device,
        mesh=finer,
        in_specs=placed,
        out_specs=(
            P(None, None, None, TA, "gz", None),
            P(None, None, None, None, TA, "gz", None),
            P(TA, "gz"),
            P(),
        ),
        check_vma=False,
    )
```

profile of v0, /device:TPU:1, one launch (start us, length us, event | category | flops | bytes accessed | tf_op | source)
XLA Modules:
  0.0 154.1 jit_solution(9629887027639376099)
XLA Ops:
  0.6 0.9 broadcast_multiply_fusion.10
  1.9 8.4 %all-gather = f32[4,3,3,4,256]{4,3,2,1,0:T(4,128)S(1)} all-gather(f32[2,3,3,4,256]{4,3,2,1,0:T(4,128)S(1)} %pad_maximum_fusion.13), channel_id=2, replica_groups=mesh['ta_0'=8,'ta_1'=4,'ta_2'=2,'gz'=8] {'ta_2'}, dimensions={0}, use_global_device_ids=true | all-gather | bytes 221184 | tf_op jit(solution)/shard_map/all_gather | solution.py:22
  10.7 9.4 %all-gather.1 = f32[8,3,3,4,256]{4,3,2,1,0:T(4,128)S(1)} all-gather(f32[2,3,3,4,256]{4,3,2,1,0:T(4,128)S(1)} %get-tuple-element.165), channel_id=3, replica_groups=mesh['ta_0'=8,'ta_1'=4,'ta_2'=2,'gz'=8] {'ta_1'}, dimensions={0}, use_global_device_ids=true | all-gather | bytes 368640 | tf_op jit(solution)/shard_map/all_gather | solution.py:22
  20.7 20.6 %all-gather.2 = f32[16,3,3,4,256]{4,3,2,1,0:T(4,128)S(1)} all-gather(f32[2,3,3,4,256]{4,3,2,1,0:T(4,128)S(1)} %get-tuple-element.159), channel_id=4, replica_groups=mesh['ta_0'=8,'ta_1'=4,'ta_2'=2,'gz'=8] {'ta_0'}, dimensions={0}, use_global_device_ids=true | all-gather | bytes 663552 | tf_op jit(solution)/shard_map/all_gather | solution.py:22
  42.9 0.6 pad_maximum_fusion.17
  43.6 7.2 %collective-permute-start = (f32[2,3,3,2,1,256]{5,3,2,1,4,0:T(2,128)}, f32[2,3,3,2,1,256]{5,3,2,1,4,0:T(2,128)}, u32[]{:S(2)}, u32[]{:S(2)}) collective-permute-start(f32[2,3,3,2,1,256]{5,3,2,1,4,0:T(2,128)} %pad_maximum_fusion.17), channel_id=1, source_target_pairs={{1,0},{2,1},{3,2},{4,3},{5,4},{6,5},{7,6},{0,7},{9,8},{10,9},{11,1... | collective-permute-start | bytes 110600 | tf_op jit(solution)/shard_map/ppermute | solution.py:35
  50.8 0.7 pad_maximum_fusion.12
  51.5 0.7 fusion.30
  53.0 0.6 slice.491
  54.0 0.6 slice.489
  54.7 1.0 copy-done.3
  55.9 0.9 neg.62
  56.8 1.5 copy.214
  58.5 0.3 reshape.231
  58.8 0.7 copy-done.26
  59.7 0.3 neg.59
  60.0 0.7 copy-done.27
  61.2 0.9 copy-done.7
  62.1 1.2 subtract_reduce_fusion.14
  63.8 0.7 pad_maximum_fusion.16
  64.5 2.4 %collective-permute-start.1 = (f32[2,2,3,3,2,1,256]{6,5,4,3,2,1,0:T(1,128)}, f32[2,2,3,3,2,1,256]{6,5,4,3,2,1,0:T(1,128)}, u32[]{:S(2)}, u32[]{:S(2)}) collective-permute-start(f32[2,2,3,3,2,1,256]{6,5,4,3,2,1,0:T(1,128)} %pad_maximum_fusion.16), channel_id=1, source_target_pairs={{1,0},{2,1},{3,2},{4,3},{5,4},{6,5},{7,6},{0,7},{9,8},{10,9},{11,1... | collective-permute-start | bytes 221192 | tf_op jit(solution)/shard_map/ppermute | solution.py:35
  66.9 0.6 fusion.1
  67.8 0.6 slice.509
  68.7 0.6 slice.507
  70.6 0.6 copy.212
  72.0 0.9 copy-done.16
  72.9 0.7 pad_maximum_fusion.10
  73.6 0.7 maximum_bitcast_fusion
  74.5 0.7 copy-done.25
  75.3 0.8 copy-done.15
  76.0 0.8 subtract_reduce_fusion.7
  76.9 0.6 slice.536
  77.6 0.7 slice.538
  78.2 0.7 slice.521
  78.9 0.7 slice.527
  79.5 0.9 mul.1834
  80.4 0.9 mul.1830
  81.3 0.7 slice_bitcast_fusion.53
  82.2 0.8 copy-done.5
  83.3 0.6 negate_bitcast_fusion
  84.6 0.6 slice.518
  85.3 0.9 slice.517
  86.3 0.6 slice.520
  87.2 0.9 mul.1880
  88.4 0.3 mul.1876
  88.7 0.8 copy-done
  89.6 0.3 mul.1853
  89.8 0.5 copy-done.28
  90.7 0.6 copy-done.20
  91.5 0.7 copy-done.11
  92.2 0.4 subtract_reduce_fusion.8
  92.6 0.5 copy-done.18
  93.3 0.8 slice_bitcast_fusion.45
  94.2 0.8 copy-done.22
  95.1 0.8 copy-done.21
  96.0 0.8 copy-done.9
  96.8 0.6 subtract_reduce_fusion.4
  97.7 1.2 fusion.29
  98.9 12.5 %psum.28 = f32[]{:T(128)} all-reduce(f32[]{:T(128)} %get-tuple-element.98), channel_id=1, replica_groups=mesh['ta_0'=8,'ta_1'=4,'ta_2'=2,'gz'=8] {'ta_0'}, use_global_device_ids=true, to_apply=%region_71.72 | all-reduce | flops 1 | bytes 8 | tf_op jit(solution)/shard_map/psum | solution.py:40
  111.4 0.7 copy.175
  112.1 8.4 %psum.29 = f32[]{:T(128)} all-reduce(f32[]{:T(128)} %psum.28), channel_id=1, replica_groups=mesh['ta_0'=8,'ta_1'=4,'ta_2'=2,'gz'=8] {'ta_1'}, use_global_device_ids=true, to_apply=%region_72.73 | all-reduce | flops 1 | bytes 8 | tf_op jit(solution)/shard_map/psum | solution.py:40
  120.5 18.5 %psum.30 = f32[]{:T(128)} all-reduce(f32[]{:T(128)} %psum.29), channel_id=1, replica_groups=mesh['ta_0'=8,'ta_1'=4,'ta_2'=2,'gz'=8] {'ta_2'}, use_global_device_ids=true, to_apply=%region_73.74 | all-reduce | flops 1 | bytes 8 | tf_op jit(solution)/shard_map/psum | solution.py:40
  138.9 0.9 pad_maximum_fusion.9
  139.8 12.5 %psum.31 = f32[]{:T(128)} all-reduce(f32[]{:T(128)} %psum.30), channel_id=1, replica_groups=mesh['ta_0'=8,'ta_1'=4,'ta_2'=2,'gz'=8] {'gz'}, use_global_device_ids=true, to_apply=%region_74.75 | all-reduce | flops 1 | bytes 8 | tf_op jit(solution)/shard_map/psum | solution.py:40
  (157 shorter events, 11.4 us)
Async XLA Ops:
  0.6 0.9 copy-start.4
  43.6 37.8 %collective-permute-start = (f32[2,3,3,2,1,256]{5,3,2,1,4,0:T(2,128)}, f32[2,3,3,2,1,256]{5,3,2,1,4,0:T(2,128)}, u32[]{:S(2)}, u32[]{:S(2)}) collective-permute-start(f32[2,3,3,2,1,256]{5,3,2,1,4,0:T(2,128)} %pad_maximum_fusion.17), channel_id=1, source_target_pairs={{1,0},{2,1},{3,2},{4,3},{5,4},{6,5},{7,6},{0,7},{9,8},{10,9},{11,1... | collective-permute-start | bytes 110600 | tf_op jit(solution)/shard_map/ppermute | solution.py:35
  54.6 1.0 copy-start.3
  58.8 0.8 copy-start.26
  60.0 0.8 copy-start.27
  61.2 0.9 copy-start.7
  61.2 0.9 copy-start.8
  62.1 1.2 copy-start.14
  64.5 28.7 %collective-permute-start.1 = (f32[2,2,3,3,2,1,256]{6,5,4,3,2,1,0:T(1,128)}, f32[2,2,3,3,2,1,256]{6,5,4,3,2,1,0:T(1,128)}, u32[]{:S(2)}, u32[]{:S(2)}) collective-permute-start(f32[2,2,3,3,2,1,256]{6,5,4,3,2,1,0:T(1,128)} %pad_maximum_fusion.16), channel_id=1, source_target_pairs={{1,0},{2,1},{3,2},{4,3},{5,4},{6,5},{7,6},{0,7},{9,8},{10,9},{11,1... | collective-permute-start | bytes 221192 | tf_op jit(solution)/shard_map/ppermute | solution.py:35
  71.9 0.9 copy-start.16
  72.0 0.9 copy-start.17
  73.6 0.8 copy-start.24
  74.4 0.8 copy-start.25
  75.1 0.9 copy-start.15
  80.4 1.8 %copy-start.13 = (f32[3,3,2,3,256]{4,3,1,0,2:T(4,128)S(1)}, f32[3,3,2,3,256]{4,3,1,0,2:T(4,128)}, u32[]{:S(2)}) copy-start(f32[3,3,2,3,256]{4,3,1,0,2:T(4,128)} %fusion.1) | copy-start | bytes 165892
  82.1 0.9 copy-start.5
  82.2 0.9 copy-start.6
  88.4 1.1 copy-start
  88.4 1.1 copy-start.29
  89.6 0.8 copy-start.28
  90.4 0.9 copy-start.20
  91.3 0.9 copy-start.11
  91.3 0.9 copy-start.12
  92.2 0.9 copy-start.18
  92.2 0.9 copy-start.19
  93.2 0.9 copy-start.23
  94.1 0.9 copy-start.22
  95.0 0.9 copy-start.21
  95.9 0.9 copy-start.9
  95.9 0.9 copy-start.10
  97.5 13.9 %copy-start.2 = (f32[2,3,3,2,4,256]{5,4,2,1,3,0:T(4,128)S(1)}, f32[2,3,3,2,4,256]{5,4,2,1,3,0:T(4,128)}, u32[]{:S(2)}) copy-start(f32[2,3,3,2,4,256]{5,4,2,1,3,0:T(4,128)} %pad_maximum_fusion.10) | copy-start | bytes 442372
  120.4 18.5 %copy-start.1 = (f32[1,2,3,3,2,4,256]{6,5,4,3,2,1,0:T(4,128)S(1)}, f32[1,2,3,3,2,4,256]{6,5,4,3,2,1,0:T(4,128)}, u32[]{:S(2)}) copy-start(f32[1,2,3,3,2,4,256]{6,5,4,3,2,1,0:T(4,128)} %maximum_bitcast_fusion) | copy-start | bytes 442372
where the time goes:
time: 156 us; the launch traced here: 154 us
  blocking collectives  90.2 us (58%)
  local copies, waits for them, and re-layouts  33.9 us (22%)
  other arithmetic  17.1 us (11%)
  starting transfers between devices  9.56 us (6%)
  between operations  3.22 us (2%)
    psum x4, blocking collectives, over_axes(): shard = lax.psum(shard, axis)  51.8 us
    all_gather x3, blocking collectives, carried_in(): pieces = lax.all_gather(so_far, axis)  38.4 us
    unnamed x63, local copies, waits for them, and re-layouts  13.1 us
    ppermute x2, starting transfers between devices, from_behind(): return lax.ppermute(block, axis, route)  9.56 us
    slice x18, local copies, waits for them, and re-layouts, shifted(): jnp.roll(lattice_grid, -1, axis=lattice_grid.ndim - 2 + direction)  6.19 us
    reduce_sum x29, other arithmetic, complex_product(): jnp.sum(first_real[:, :, None] * second_real[None] - first_imag[:, :, Non...  6.1 us
    neg x6, local copies, waits for them, and re-layouts, dagger(): -jnp.swapaxes(matrix_pair[1], 0, 1)  3.62 us
  transfers between devices with their start and end apart: 2, of which 0 were waited for; matrix products, arithmetic and copies ran while one was open for 19% of the time, Pallas kernels for 0%

commit v1 on v0

v1 whole, which is shorter than its diff:
```python
import jax
import jax.numpy as jnp
from jax import lax
from jax.experimental import pallas as pl
from jax.experimental.pallas import tpu as pltpu
from jax.sharding import PartitionSpec as P

ROWS = 8
LANES = 128
Y = 16
PLANES = 4
HALO_ROWS = (3, 7)
MESH = pl.DeviceIdType.MESH
F32 = jnp.float32


def mul(a, b):
    ar, ai = a
    br, bi = b
    re = im = None
    for k in range(3):
        xr, xi = ar[:, k][:, None], ai[:, k][:, None]
        yr, yi = br[k][None], bi[k][None]
        r = xr * yr - xi * yi
        i = xr * yi + xi * yr
        re, im = (r, i) if re is None else (re + r, im + i)
    return re, im


def mul_dagger(a, b):
    ar, ai = a
    br, bi = b
    re = im = None
    for k in range(3):
        xr, xi = ar[:, k][:, None], ai[:, k][:, None]
        yr, yi = br[:, k][None], bi[:, k][None]
        r = xr * yr + xi * yi
        i = xi * yr - xr * yi
        re, im = (r, i) if re is None else (re + r, im + i)
    return re, im


def both(fn, pair):
    return fn(pair[0]), fn(pair[1])


def rows_of(shape):
    return lax.broadcasted_iota(jnp.int32, shape, len(shape) - 2)


def lanes_of(shape):
    return lax.broadcasted_iota(jnp.int32, shape, len(shape) - 1)


def pick(mask, a, b):
    return jnp.where(mask, a[0], b[0]), jnp.where(mask, a[1], b[1])


def ahead_x(pair):
    def shift(v):
        near = pltpu.roll(v, LANES - Y, v.ndim - 1)
        far = pltpu.roll(near, PLANES, v.ndim - 2)
        return jnp.where(lanes_of(v.shape) >= LANES - Y, far, near)

    return both(shift, pair)


def ahead_y(pair):
    def shift(v):
        near = pltpu.roll(v, LANES - 1, v.ndim - 1)
        wrap = pltpu.roll(v, Y - 1, v.ndim - 1)
        return jnp.where(lanes_of(v.shape) % Y == Y - 1, wrap, near)

    return both(shift, pair)


def ahead_z(pair, halo):
    def shift(v, h):
        near = pltpu.roll(v, ROWS - 1, v.ndim - 2)
        return jnp.where(rows_of(v.shape) % PLANES == PLANES - 1, h, near)

    return shift(pair[0], halo[0]), shift(pair[1], halo[1])


def or_unit(mask, pair):
    re, im = pair
    return (
        jnp.stack(
            [
                jnp.stack([jnp.where(mask, re[i, j], 1.0 if i == j else 0.0) for j in range(3)])
                for i in range(3)
            ]
        ),
        jnp.where(mask, im, 0.0),
    )


def row_of(ref, row):
    return ref.at[:, :, :, pl.ds(row, 1), :]


def load(ref):
    return ref[0], ref[1]


def kernel(
    time_ref, space_ref, gauge_ref, fixed_ref, profile_ref, mean_ref,
    tl, sl, total, scanned, spread, in1, in2, carry, carry_halo, time_halo, space_halo,
    g_out, v_out, part, part_in,
    load_sem, store_sem, halo_send, halo_recv,
    send1, recv1, send2, recv2, send3, recv3, send4, recv4, send_part, recv_part,
):
    me = lax.axis_index("ta")
    z = lax.axis_index("gz")
    group, member = me // ROWS, me % ROWS
    below = (z + 7) % 8

    def in_row(k):
        return group * ROWS + (member + k) % ROWS, z

    def in_column(k):
        return (group + k) % ROWS * ROWS + member, z

    def in_height(k):
        return me, (z + k) % ROWS

    barrier = pltpu.get_barrier_semaphore()
    for k in range(1, ROWS):
        for device in (in_row(k), in_column(k), in_height(k)):
            pl.semaphore_signal(barrier, inc=1, device_id=device, device_id_type=MESH)

    loads = []
    for c in range(2):
        loads.append(pltpu.make_async_copy(
            time_ref.at[:, :, :, :, :, pl.ds(c * LANES, LANES)],
            tl.at[:, :, :, :, pl.ds(c * PLANES, PLANES), :],
            load_sem.at[c],
        ))
    for c in range(2):
        loads.append(pltpu.make_async_copy(
            space_ref.at[:, :, :, :, :, :, pl.ds(c * LANES, LANES)],
            sl.at[:, :, :, :, :, pl.ds(c * PLANES, PLANES), :],
            load_sem.at[2 + c],
        ))
    for copy in loads:
        copy.start()
    loads[0].wait()
    loads[1].wait()

    def time_link(t):
        return tl[0, :, :, t], tl[1, :, :, t]

    def space_link(mu, t):
        return sl[mu, 0, :, :, t], sl[mu, 1, :, :, t]

    prod = mul(time_link(0), time_link(1))
    total[0], total[1] = prod
    pl.semaphore_wait(barrier, 3 * (ROWS - 1))

    def remote(src, dst, send, recv, device):
        return pltpu.make_async_remote_copy(
            src_ref=src, dst_ref=dst, send_sem=send, recv_sem=recv,
            device_id=device, device_id_type=MESH,
        )

    first = []
    for k in range(1, ROWS):
        first.append(remote(
            row_of(total, (member + k) % ROWS), row_of(in1, member),
            send1.at[k], recv1.at[k], in_row(k),
        ))
    for copy in first:
        copy.start()

    loads[2].wait()
    loads[3].wait()
    halos = []
    for c in range(2):
        for mu in range(2):
            halos.append(remote(
                sl.at[mu, :, :, :, :, pl.ds(c * PLANES, 1), :],
                space_halo.at[mu, :, :, :, :, pl.ds(HALO_ROWS[c], 1), :],
                halo_send.at[c * 2 + mu], halo_recv.at[c * 2 + mu], (me, below),
            ))
    for c in range(2):
        halos.append(remote(
            tl.at[:, :, :, 0, pl.ds(c * PLANES, 1), :],
            time_halo.at[:, :, :, pl.ds(HALO_ROWS[c], 1), :],
            halo_send.at[4 + c], halo_recv.at[4 + c], (me, below),
        ))
    for copy in halos:
        copy.start()

    rows = rows_of((ROWS, LANES))
    for copy in first:
        copy.wait_recv()
    scan = pick(rows == member, load(total), load(in1))
    for s in (1, 2, 4):
        earlier = both(lambda v: pltpu.roll(v, s, 2), scan)
        scan = pick(rows >= s, mul(earlier, scan), scan)
    scanned[0], scanned[1] = scan

    second = []
    for k in range(1, ROWS):
        second.append(remote(
            row_of(scanned, ROWS - 1), row_of(in2, group),
            send2.at[k], recv2.at[k], in_column(k),
        ))
    for copy in second:
        copy.start()

    for copy in halos:
        copy.wait_recv()
    sites = jnp.zeros((ROWS, LANES), F32)
    lanes = lanes_of((ROWS, LANES))
    for t in range(2):
        density = jnp.zeros((ROWS, LANES), F32)
        for mu, nu in ((0, 1), (0, 2), (1, 2)):
            along_mu, along_nu = space_link(mu, t), space_link(nu, t)
            nu_moved = ahead_x(along_nu) if mu == 0 else ahead_y(along_nu)
            if nu == 1:
                mu_moved = ahead_y(along_mu)
            else:
                mu_moved = ahead_z(
                    along_mu, (space_halo[mu, 0, :, :, t], space_halo[mu, 1, :, :, t])
                )
            there, back = mul(along_mu, nu_moved), mul(along_nu, mu_moved)
            trace = jnp.sum(there[0] * back[0] + there[1] * back[1], axis=(0, 1))
            density = density + (1.0 - trace / 3.0)
        of_row = jnp.sum(density, axis=1, keepdims=True)
        spots = jnp.where(lanes == rows % PLANES, of_row, 0.0)
        profile = jnp.sum(spots, axis=0, keepdims=True) * (1.0 / (3 * 2 * LANES))
        profile_ref[t : t + 1, :] = profile[:, :PLANES]
        sites = sites + density
    part[0] = jnp.broadcast_to(jnp.sum(sites, axis=0, keepdims=True), (ROWS, LANES))

    def add_up(stage, place, partner):
        copies = []
        for k in range(1, ROWS):
            copies.append(remote(
                part.at[stage, pl.ds(0, 1), :], part_in.at[stage, pl.ds(place, 1), :],
                send_part.at[stage, k], recv_part.at[stage, k], partner(k),
            ))
        for copy in copies:
            copy.start()
        return copies

    def added(stage, place, copies):
        for copy in copies:
            copy.wait_recv()
        parts = jnp.where(rows == place, part[stage], part_in[stage])
        return jnp.broadcast_to(jnp.sum(parts, axis=0, keepdims=True), (ROWS, LANES))

    stage0 = add_up(0, member, in_row)

    for copy in second:
        copy.wait_recv()
    before = or_unit(rows < group, load(in2))
    for s in (1, 2, 4):
        before = mul(before, both(lambda v: pltpu.roll(v, ROWS - s, 2), before))
    before = both(lambda v: jnp.broadcast_to(v[:, :, 0:1], v.shape), before)
    inside = both(lambda v: pltpu.roll(v, 1, 2), scan)
    start = mul(before, or_unit(rows >= 1, inside))
    spread[0], spread[1] = start

    third = []
    for k in range(1, ROWS):
        third.append(remote(
            row_of(spread, (member + k) % ROWS), row_of(carry, member),
            send3.at[k], recv3.at[k], in_row(k),
        ))
    for copy in third:
        copy.start()
    lowest = member % PLANES == 0
    for k in range(ROWS):
        @pl.when(lowest)
        def _(k=k):
            remote(
                row_of(spread, k), row_of(carry_halo, member + PLANES - 1),
                send4.at[k], recv4.at[member // PLANES], (group * ROWS + k, below),
            ).start()

    part[1] = added(0, member, stage0)
    stage1 = add_up(1, z, in_height)

    for copy in third:
        copy.wait_recv()
    g0 = pick(rows == member, load(spread), load(carry))
    g1 = mul(g0, time_link(0))
    g = (g0, g1)
    for t in range(2):
        g_out[0, :, :, t], g_out[1, :, :, t] = g[t]

    stores = []

    def store(src, dst):
        for c in range(2):
            copy = pltpu.make_async_copy(
                src(pl.ds(c * PLANES, PLANES)), dst(pl.ds(c * LANES, LANES)),
                store_sem.at[len(stores)],
            )
            copy.start()
            stores.append(copy)

    store(lambda q: g_out.at[:, :, :, :, q, :], lambda q: gauge_ref.at[:, :, :, :, :, q])

    def fix(mu, t, ahead):
        v = mul_dagger(mul(g[t], space_link(mu, t)), ahead)
        v_out[mu, 0, :, :, t], v_out[mu, 1, :, :, t] = v

    def store_fixed(mu):
        store(
            lambda q: v_out.at[mu, :, :, :, :, q, :],
            lambda q: fixed_ref.at[mu, :, :, :, :, :, q],
        )

    for t in range(2):
        fix(0, t, ahead_x(g[t]))
    store_fixed(0)
    for t in range(2):
        fix(1, t, ahead_y(g[t]))
    store_fixed(1)
    for c in range(2):
        remote(
            row_of(spread, 0), row_of(carry_halo, HALO_ROWS[c]),
            send4.at[c], recv4.at[c], (me, below),
        ).wait_recv()
    g0z = ahead_z(g0, load(carry_halo))
    g1z = mul(g0z, ahead_z(time_link(0), load(time_halo)))
    for t, ahead in ((0, g0z), (1, g1z)):
        fix(2, t, ahead)
    store_fixed(2)

    part[2] = added(1, z, stage1)
    stage2 = add_up(2, group, in_column)
    whole = added(2, group, stage2)
    mean = jnp.sum(whole[0:1], axis=1, keepdims=True)
    mean_ref[...] = mean * (1.0 / (3 * 2 * LANES * 4096))

    for copy in stores:
        copy.wait()
    for copy in first + halos + second + stage0 + third + stage1 + stage2:
        copy.wait_send()
    for k in range(ROWS):
        @pl.when(lowest)
        def _(k=k):
            remote(
                row_of(spread, k), row_of(carry_halo, member + PLANES - 1),
                send4.at[k], recv4.at[member // PLANES], (group * ROWS + k, below),
            ).wait_send()


def on_device(time_links, space_links):
    pair = (2, 3, 3, ROWS, LANES)
    dma = pltpu.SemaphoreType.DMA
    gauge, fixed, profile, mean = pl.pallas_call(
        kernel,
        out_shape=(
            jax.ShapeDtypeStruct(time_links.shape, F32),
            jax.ShapeDtypeStruct(space_links.shape, F32),
            jax.ShapeDtypeStruct((2, PLANES), F32),
            jax.ShapeDtypeStruct((1, 1), F32),
        ),
        in_specs=[pl.BlockSpec(memory_space=pl.ANY)] * 2,
        out_specs=(
            pl.BlockSpec(memory_space=pl.ANY),
            pl.BlockSpec(memory_space=pl.ANY),
            pl.BlockSpec(memory_space=pltpu.VMEM),
            pl.BlockSpec(memory_space=pltpu.VMEM),
        ),
        scratch_shapes=[
            pltpu.VMEM((2, 3, 3, 2, ROWS, LANES), F32),
            pltpu.VMEM((3, 2, 3, 3, 2, ROWS, LANES), F32),
            pltpu.VMEM(pair, F32),
            pltpu.VMEM(pair, F32),
            pltpu.VMEM(pair, F32),
            pltpu.VMEM(pair, F32),
            pltpu.VMEM(pair, F32),
            pltpu.VMEM(pair, F32),
            pltpu.VMEM(pair, F32),
            pltpu.VMEM(pair, F32),
            pltpu.VMEM((2, 2, 3, 3, 2, ROWS, LANES), F32),
            pltpu.VMEM((2, 3, 3, 2, ROWS, LANES), F32),
            pltpu.VMEM((3, 2, 3, 3, 2, ROWS, LANES), F32),
            pltpu.VMEM((3, ROWS, LANES), F32),
            pltpu.VMEM((3, ROWS, LANES), F32),
            dma((4,)), dma((8,)), dma((6,)), dma((6,)),
            dma((ROWS,)), dma((ROWS,)), dma((ROWS,)), dma((ROWS,)),
            dma((ROWS,)), dma((ROWS,)), dma((ROWS,)), dma((2,)),
            dma((3, ROWS)), dma((3, ROWS)),
        ],
        compiler_params=pltpu.CompilerParams(collective_id=0, has_side_effects=True),
    )(time_links, space_links)
    return gauge, fixed, profile, mean.reshape(())


def solution(mesh):
    placed = (P(None, None, None, "ta", "gz", None), P(None, None, None, None, "ta", "gz", None))
    return jax.shard_map(
        on_device,
        mesh=mesh,
        in_specs=placed,
        out_specs=(*placed, P("ta", "gz"), P()),
        check_vma=False,
    )
```

time: 156 us -> 40.7 us (0.26)
  the two profiles are of different devices: /device:TPU:1 before, /device:TPU:64 now
where the time goes in v1:
time: 40.7 us; the launch traced here: 40.5 us
  Pallas kernels  34.2 us (84%)
  local copies, waits for them, and re-layouts  3.95 us (10%)
  between operations  2.34 us (6%)
    pallas_call x1, Pallas kernels, on_device(): pl.pallas_call(kernel, out_shape=(jax.ShapeDtypeStruct(time_links.shape,...  34.2 us
    unnamed x5, local copies, waits for them, and re-layouts  3.95 us

profile of v1, /device:TPU:64, one launch (start us, length us, event | category | flops | bytes accessed | tf_op | source)
XLA Modules:
  0.0 40.5 jit_solution(6560375595918078566)
XLA Ops:
  0.6 34.2 %shard_map.57 = (f32[2,3,3,2,4,256]{5,4,3,2,1,0:T(4,128)}, f32[3,2,3,3,2,4,256]{6,5,4,3,2,1,0:T(4,128)}, f32[2,4]{1,0:T(2,128)}, f32[1,1]{1,0:T(1,128)}) custom-call(f32[2,3,3,2,4,256]{5,4,3,2,1,0:T(4,128)} %time_ref.1, f32[3,2,3,3,2,4,256]{6,5,4,3,2,1,0:T(4,128)} %space_ref.1), custom_call_target="tpu_custom_call" | custom-call | tf_op jit(solution)/shard_map/pallas_call | solution.py:356
  34.9 1.6 %copy.10 = f32[2,3,3,2,4,256]{5,4,3,2,1,0:T(4,128)} copy(f32[2,3,3,2,4,256]{5,4,3,2,1,0:T(4,128)} %get-tuple-element.16) | data formatting | bytes 294912
  36.4 0.0 copy-start
  36.5 1.8 %copy.11 = f32[3,2,3,3,2,4,256]{6,5,4,3,2,1,0:T(4,128)} copy(f32[3,2,3,3,2,4,256]{6,5,4,3,2,1,0:T(4,128)} %get-tuple-element.17) | data formatting | bytes 884736
  38.3 0.0 copy-done
  38.3 0.6 %copy.12 = f32[2,4]{1,0:T(2,128)} copy(f32[2,4]{1,0:T(2,128)S(1)} %copy-done) | data formatting | bytes 64
Async XLA Ops:
  36.4 1.8 %copy-start = (f32[2,4]{1,0:T(2,128)S(1)}, f32[2,4]{1,0:T(2,128)}, u32[]{:S(2)}) copy-start(f32[2,4]{1,0:T(2,128)} %get-tuple-element.18) | copy-start | bytes 100

commit v2 on v1

v2 whole, which is shorter than its diff:
```python
import jax
import jax.numpy as jnp
from jax import lax
from jax.experimental import pallas as pl
from jax.experimental.pallas import tpu as pltpu
from jax.sharding import PartitionSpec as P

ROWS = 8
LANES = 128
Y = 16
PLANES = 4
HALO_ROWS = (3, 7)
EARLY = 4
DEPTH = 8
MESH = pl.DeviceIdType.MESH
F32 = jnp.float32


def mul(a, b):
    ar, ai = a
    br, bi = b
    re = im = None
    for k in range(3):
        xr, xi = ar[:, k][:, None], ai[:, k][:, None]
        yr, yi = br[k][None], bi[k][None]
        r = xr * yr - xi * yi
        i = xr * yi + xi * yr
        re, im = (r, i) if re is None else (re + r, im + i)
    return re, im


def mul_dagger(a, b):
    ar, ai = a
    br, bi = b
    re = im = None
    for k in range(3):
        xr, xi = ar[:, k][:, None], ai[:, k][:, None]
        yr, yi = br[:, k][None], bi[:, k][None]
        r = xr * yr + xi * yi
        i = xi * yr - xr * yi
        re, im = (r, i) if re is None else (re + r, im + i)
    return re, im


def dagger_mul(a, b):
    ar, ai = a
    br, bi = b
    re = im = None
    for k in range(3):
        xr, xi = ar[k][:, None], ai[k][:, None]
        yr, yi = br[k][None], bi[k][None]
        r = xr * yr + xi * yi
        i = xr * yi - xi * yr
        re, im = (r, i) if re is None else (re + r, im + i)
    return re, im


def overlap(a, b):
    return jnp.sum(a[0] * b[0] + a[1] * b[1], axis=(0, 1))


def both(fn, pair):
    return fn(pair[0]), fn(pair[1])


def rows_of(shape):
    return lax.broadcasted_iota(jnp.int32, shape, len(shape) - 2)


def lanes_of(shape):
    return lax.broadcasted_iota(jnp.int32, shape, len(shape) - 1)


def pick(mask, a, b):
    return jnp.where(mask, a[0], b[0]), jnp.where(mask, a[1], b[1])


def ahead_x(pair):
    def shift(v):
        near = pltpu.roll(v, LANES - Y, v.ndim - 1)
        far = pltpu.roll(near, PLANES, v.ndim - 2)
        return jnp.where(lanes_of(v.shape) >= LANES - Y, far, near)

    return both(shift, pair)


def ahead_y(pair):
    def shift(v):
        near = pltpu.roll(v, LANES - 1, v.ndim - 1)
        wrap = pltpu.roll(v, Y - 1, v.ndim - 1)
        return jnp.where(lanes_of(v.shape) % Y == Y - 1, wrap, near)

    return both(shift, pair)


def up_z(pair):
    return both(lambda v: pltpu.roll(v, ROWS - 1, v.ndim - 2), pair)


def ahead_z(pair, halo):
    top = rows_of((ROWS, LANES)) % PLANES == PLANES - 1
    return pick(top, halo, up_z(pair))


def or_unit(mask, pair):
    re, im = pair
    return (
        jnp.stack(
            [
                jnp.stack([jnp.where(mask, re[i, j], 1.0 if i == j else 0.0) for j in range(3)])
                for i in range(3)
            ]
        ),
        jnp.where(mask, im, 0.0),
    )


def row_of(ref, row):
    return ref.at[:, :, :, pl.ds(row, 1), :]


def load(ref):
    return ref[0], ref[1]


def kernel(
    time_ref, space_ref, g_out, v_out, profile_ref, mean_ref,
    tl, sl, total, scanned, spread, in1, in2, carry, carry_halo, time_halo, space_halo,
    around, part, part_row, part_all, part_back,
    load_sem, halo_send, halo_recv,
    send1, recv1, send2, recv2, send3, recv3, send4, recv4,
    send_row, recv_row, send_all, recv_all, send_back, recv_back,
):
    me = lax.axis_index("ta")
    z = lax.axis_index("gz")
    group, member = me // ROWS, me % ROWS
    below, above = (z + DEPTH - 1) % DEPTH, (z + 1) % DEPTH
    early = z < EARLY

    def in_row(k):
        return group * ROWS + (member + k) % ROWS, z

    def in_column(k, height=z):
        return (group + k) % ROWS * ROWS + member, height

    space_loads, time_loads = [], []
    for c in range(2):
        space_loads.append(pltpu.make_async_copy(
            space_ref.at[:, :, :, :, :, :, pl.ds(c * LANES, LANES)],
            sl.at[:, :, :, :, :, pl.ds(c * PLANES, PLANES), :],
            load_sem.at[c],
        ))
    for c in range(2):
        time_loads.append(pltpu.make_async_copy(
            time_ref.at[:, :, :, :, :, pl.ds(c * LANES, LANES)],
            tl.at[:, :, :, :, pl.ds(c * PLANES, PLANES), :],
            load_sem.at[2 + c],
        ))
    for copy in space_loads + time_loads:
        copy.start()

    barrier = pltpu.get_barrier_semaphore()

    def greet(device):
        pl.semaphore_signal(barrier, inc=1, device_id=device, device_id_type=MESH)

    for k in range(1, ROWS):
        greet(in_row(k))

    @pl.when(early)
    def _():
        for k in range(1, DEPTH):
            greet((me, (z + k) % DEPTH))

        def to_column(k, carried):
            for height in range(DEPTH):
                greet(in_column(k, height))
            return carried

        lax.fori_loop(1, ROWS, to_column, 0)

    @pl.when(jnp.logical_not(early))
    def _():
        for k in range(1, ROWS):
            greet(in_column(k))
        greet((me, above))

    def time_link(t):
        return tl[0, :, :, t], tl[1, :, :, t]

    def space_link(mu, t):
        return sl[mu, 0, :, :, t], sl[mu, 1, :, :, t]

    def remote(src, dst, send, recv, device):
        return pltpu.make_async_remote_copy(
            src_ref=src, dst_ref=dst, send_sem=send, recv_sem=recv,
            device_id=device, device_id_type=MESH,
        )

    for copy in space_loads:
        copy.wait()
    late_below = jnp.logical_or(z == 0, z > EARLY).astype(jnp.int32)
    of_column = jnp.where(early, EARLY * ROWS - 1, EARLY * ROWS + ROWS - 1)
    pl.semaphore_wait(barrier, ROWS - 1 + of_column + late_below)

    halos = []
    for mu in range(2):
        for c in range(2):
            halos.append(remote(
                sl.at[mu, :, :, :, :, pl.ds(c * PLANES, 1), :],
                space_halo.at[mu, :, :, :, :, pl.ds(HALO_ROWS[c], 1), :],
                halo_send.at[c * 2 + mu], halo_recv.at[c * 2 + mu], (me, below),
            ))
    for copy in halos:
        copy.start()

    for copy in time_loads:
        copy.wait()
    prod = mul(time_link(0), time_link(1))
    total[0], total[1] = prod

    first = []
    for k in range(1, ROWS):
        first.append(remote(
            row_of(total, (member + k) % ROWS), row_of(in1, member),
            send1.at[k], recv1.at[k], in_row(k),
        ))
    for copy in first:
        copy.start()
    time_halos = []
    for c in range(2):
        time_halos.append(remote(
            tl.at[:, :, :, 0, pl.ds(c * PLANES, 1), :],
            time_halo.at[:, :, :, pl.ds(HALO_ROWS[c], 1), :],
            halo_send.at[4 + c], halo_recv.at[4 + c], (me, below),
        ))
    for copy in time_halos:
        copy.start()

    rows = rows_of((ROWS, LANES))
    lanes = lanes_of((ROWS, LANES))
    top = rows % PLANES == PLANES - 1
    traces = []
    for t in range(2):
        ux, uy, uz = (space_link(mu, t) for mu in range(3))
        trace = overlap(mul(ux, ahead_x(uy)), mul(uy, ahead_y(ux)))
        for mu, along, ahead in ((0, ux, ahead_x), (1, uy, ahead_y)):
            rest = dagger_mul(uz, mul(along, ahead(uz)))
            around[mu, 0, :, :, t], around[mu, 1, :, :, t] = rest
            trace = trace + jnp.where(top, 0.0, overlap(rest, up_z(along)))
        traces.append(trace)
    for copy in halos:
        copy.wait_recv()
    densities = []
    for t in range(2):
        trace = traces[t]
        for mu in range(2):
            rest = around[mu, 0, :, :, t], around[mu, 1, :, :, t]
            beyond = space_halo[mu, 0, :, :, t], space_halo[mu, 1, :, :, t]
            trace = trace + jnp.where(top, overlap(rest, beyond), 0.0)
        densities.append(3.0 - trace * (1.0 / 3.0))

    def spread_sum(v):
        return jnp.broadcast_to(jnp.sum(v, axis=0, keepdims=True), (ROWS, LANES))

    part[0] = spread_sum(densities[0] + densities[1])
    row_parts = []
    for k in range(1, ROWS):
        row_parts.append(remote(
            part.at[0, pl.ds(0, 1), :], part_row.at[pl.ds(member, 1), :],
            send_row.at[k], recv_row.at[k], in_row(k),
        ))
    for copy in row_parts:
        copy.start()

    for t in range(2):
        of_row = jnp.sum(densities[t], axis=1, keepdims=True)
        spots = jnp.where(lanes == rows % PLANES, of_row, 0.0)
        profile = jnp.sum(spots, axis=0, keepdims=True) * (1.0 / (3 * 2 * LANES))
        profile_ref[t : t + 1, :] = profile[:, :PLANES]

    for copy in first:
        copy.wait_recv()
    scan = pick(rows == member, load(total), load(in1))
    for s in (1, 2, 4):
        earlier = both(lambda v: pltpu.roll(v, s, 2), scan)
        scan = pick(rows >= s, mul(earlier, scan), scan)
    scanned[0], scanned[1] = scan

    def to_later(k):
        return remote(
            row_of(scanned, ROWS - 1), row_of(in2, group),
            send2.at[k], recv2.at[k], in_column(k),
        )

    for k in range(ROWS - 1, 0, -1):
        @pl.when(group + k < ROWS)
        def _(k=k):
            to_later(k).start()

    for copy in row_parts:
        copy.wait_recv()
    part[1] = spread_sum(jnp.where(rows == member, part[0], part_row[...]))

    def to_early(k, height):
        return remote(
            part.at[1, pl.ds(0, 1), :], part_all.at[group, pl.ds(z, 1), :],
            send_all.at[k, height], recv_all.at[k, z], in_column(k, height),
        )

    def each_early(act):
        for height in range(EARLY):
            @pl.when(z != height)
            def _(height=height):
                act(to_early(0, height))

        def at(k, carried):
            for height in range(EARLY):
                act(to_early(k, height))
            return carried

        lax.fori_loop(1, ROWS, at, 0)

    each_early(lambda copy: copy.start())

    inside = or_unit(rows >= 1, both(lambda v: pltpu.roll(v, 1, 2), scan))
    for k in range(1, ROWS):
        @pl.when(group >= k)
        def _(k=k):
            to_later(k).wait_recv()
    before = or_unit(rows < group, load(in2))
    for s in (1, 2, 4):
        before = mul(before, both(lambda v: pltpu.roll(v, ROWS - s, 2), before))
    before = both(lambda v: jnp.broadcast_to(v[:, :, 0:1], v.shape), before)
    spread[0], spread[1] = mul(before, inside)

    third = []
    for k in range(1, ROWS):
        third.append(remote(
            row_of(spread, (member + k) % ROWS), row_of(carry, member),
            send3.at[k], recv3.at[k], in_row(k),
        ))
    for copy in third:
        copy.start()
    lowest = member % PLANES == 0

    def to_below(k):
        return remote(
            row_of(spread, k), row_of(carry_halo, member + PLANES - 1),
            send4.at[k], recv4.at[member // PLANES], (group * ROWS + k, below),
        )

    for k in range(ROWS):
        @pl.when(lowest)
        def _(k=k):
            to_below(k).start()

    for copy in third:
        copy.wait_recv()
    g0 = pick(rows == member, load(spread), load(carry))
    g1 = mul(g0, time_link(0))
    g = (g0, g1)
    for t in range(2):
        g_out[0, :, :, t], g_out[1, :, :, t] = g[t]

    def fix(mu, t, ahead):
        v = mul_dagger(mul(g[t], space_link(mu, t)), ahead)
        v_out[mu, 0, :, :, t], v_out[mu, 1, :, :, t] = v

    for t in range(2):
        fix(0, t, ahead_x(g[t]))
    for t in range(2):
        fix(1, t, ahead_y(g[t]))
    for copy in time_halos:
        copy.wait_recv()
    for c in range(2):
        remote(
            row_of(spread, 0), row_of(carry_halo, HALO_ROWS[c]),
            send4.at[c], recv4.at[c], (me, below),
        ).wait_recv()
    g0z = ahead_z(g0, load(carry_halo))
    g1z = mul(g0z, ahead_z(time_link(0), load(time_halo)))
    for t, ahead in ((0, g0z), (1, g1z)):
        fix(2, t, ahead)

    def to_late():
        return remote(
            part.at[2], part_back, send_back.at[0], recv_back.at[0], (me, (z + EARLY) % DEPTH)
        )

    def write_mean(sites):
        mean = jnp.sum(sites[0:1], axis=1, keepdims=True)
        mean_ref[...] = mean * (1.0 / (3 * 2 * LANES * 4096))

    @pl.when(early)
    def _():
        for height in range(DEPTH):
            @pl.when(z != height)
            def _(height=height):
                remote(
                    part.at[1, pl.ds(0, 1), :], part_all.at[0, pl.ds(0, 1), :],
                    send_all.at[0, 0], recv_all.at[0, height], (me, below),
                ).wait_recv()

        def one(k, carried):
            for height in range(DEPTH):
                remote(
                    part.at[1, pl.ds(0, 1), :], part_all.at[0, pl.ds(0, 1), :],
                    send_all.at[0, 0], recv_all.at[k, height], (me, below),
                ).wait_recv()
            return carried

        lax.fori_loop(1, ROWS, one, 0)
        parts = None
        for k in range(ROWS):
            mine = jnp.logical_and(rows == z, group == k)
            got = jnp.where(mine, part[1], part_all[k])
            parts = got if parts is None else parts + got
        whole = spread_sum(parts)
        part[2] = whole
        to_late().start()
        write_mean(whole)
        to_late().wait_send()

    @pl.when(jnp.logical_not(early))
    def _():
        to_late().wait_recv()
        write_mean(part_back[...])

    for copy in halos + first + time_halos + row_parts + third:
        copy.wait_send()
    for k in range(1, ROWS):
        @pl.when(group + k < ROWS)
        def _(k=k):
            to_later(k).wait_send()
    each_early(lambda copy: copy.wait_send())
    for k in range(ROWS):
        @pl.when(lowest)
        def _(k=k):
            to_below(k).wait_send()


def write_out(g_out, v_out, profile, mean, gauge_ref, fixed_ref, profile_ref, mean_ref, sem):
    copies = []
    for c in range(2):
        planes, lanes = pl.ds(c * PLANES, PLANES), pl.ds(c * LANES, LANES)
        for src, dst in (
            (v_out.at[:, :, :, :, :, planes, :], fixed_ref.at[:, :, :, :, :, :, lanes]),
            (g_out.at[:, :, :, :, planes, :], gauge_ref.at[:, :, :, :, :, lanes]),
        ):
            copies.append(pltpu.make_async_copy(src, dst, sem.at[len(copies)]))
    for src, dst in ((profile, profile_ref), (mean, mean_ref)):
        copies.append(pltpu.make_async_copy(src, dst, sem.at[len(copies)]))
    for copy in copies:
        copy.start()
    for copy in copies:
        copy.wait()


def on_device(time_links, space_links):
    pair = (2, 3, 3, ROWS, LANES)
    dma = pltpu.SemaphoreType.DMA
    vmem = pl.BlockSpec(memory_space=pltpu.VMEM)
    anywhere = pl.BlockSpec(memory_space=pl.ANY)
    staged = pl.pallas_call(
        kernel,
        out_shape=(
            pltpu.VMEM((2, 3, 3, 2, ROWS, LANES), F32),
            pltpu.VMEM((3, 2, 3, 3, 2, ROWS, LANES), F32),
            pltpu.VMEM((2, PLANES), F32),
            pltpu.VMEM((1, 1), F32),
        ),
        in_specs=[pl.BlockSpec(memory_space=pltpu.HBM)] * 2,
        out_specs=(vmem,) * 4,
        scratch_shapes=[
            pltpu.VMEM((2, 3, 3, 2, ROWS, LANES), F32),
            pltpu.VMEM((3, 2, 3, 3, 2, ROWS, LANES), F32),
            *[pltpu.VMEM(pair, F32)] * 8,
            pltpu.VMEM((2, 2, 3, 3, 2, ROWS, LANES), F32),
            pltpu.VMEM((2, 2, 3, 3, 2, ROWS, LANES), F32),
            pltpu.VMEM((3, ROWS, LANES), F32),
            pltpu.VMEM((ROWS, LANES), F32),
            pltpu.VMEM((ROWS, DEPTH, LANES), F32),
            pltpu.VMEM((ROWS, LANES), F32),
            dma((4,)), dma((6,)), dma((6,)),
            dma((ROWS,)), dma((ROWS,)), dma((ROWS,)), dma((ROWS,)),
            dma((ROWS,)), dma((ROWS,)), dma((ROWS,)), dma((2,)),
            dma((ROWS,)), dma((ROWS,)), dma((ROWS, EARLY)), dma((ROWS, DEPTH)),
            dma((1,)), dma((1,)),
        ],
        compiler_params=pltpu.CompilerParams(collective_id=0, has_side_effects=True),
    )(time_links, space_links)
    gauge, fixed, profile, mean = pl.pallas_call(
        write_out,
        out_shape=(
            jax.ShapeDtypeStruct(time_links.shape, F32),
            jax.ShapeDtypeStruct(space_links.shape, F32),
            jax.ShapeDtypeStruct((2, PLANES), F32),
            jax.ShapeDtypeStruct((1, 1), F32),
        ),
        in_specs=[vmem] * 4,
        out_specs=(anywhere,) * 4,
        scratch_shapes=[dma((6,))],
        compiler_params=pltpu.CompilerParams(vmem_limit_bytes=4 * 2**20),
    )(*staged)
    return gauge, fixed, profile, mean.reshape(())


def solution(mesh):
    placed = (P(None, None, None, "ta", "gz", None), P(None, None, None, None, "ta", "gz", None))
    return jax.shard_map(
        on_device,
        mesh=mesh,
        in_specs=placed,
        out_specs=(*placed, P("ta", "gz"), P()),
        check_vma=False,
    )
```

time: 40.7 us -> 32.4 us (0.80)
  the two profiles are of different devices: /device:TPU:64 before, /device:TPU:1 now
where the time goes in v2:
time: 32.4 us; the launch traced here: 32.3 us
  Pallas kernels  31.7 us (98%)
  between operations  0.64 us (2%)
    pallas_call x1, Pallas kernels, on_device(): pl.pallas_call(kernel, out_shape=(pltpu.VMEM((2, 3, 3, 2, ROWS, LANES), F...  30.2 us
    pallas_call x1, Pallas kernels, on_device(): pl.pallas_call(write_out, out_shape=(jax.ShapeDtypeStruct(time_links.shap...  1.49 us

profile of v2, /device:TPU:1, one launch (start us, length us, event | category | flops | bytes accessed | tf_op | source)
XLA Modules:
  0.0 32.3 jit_solution(3143071724728256970)
XLA Ops:
  0.6 30.2 %shard_map.57 = (f32[2,3,3,2,8,128]{5,4,3,2,1,0:T(8,128)S(1)}, f32[3,2,3,3,2,8,128]{6,5,4,3,2,1,0:T(8,128)S(1)}, f32[2,4]{1,0:T(2,128)S(1)}, f32[1,1]{1,0:T(1,128)}) custom-call(f32[2,3,3,2,4,256]{5,4,3,2,1,0:T(4,128)} %time_ref.1, f32[3,2,3,3,2,4,256]{6,5,4,3,2,1,0:T(4,128)} %space_ref.1), custom_call_target="tpu_custom_call" | custom-call | tf_op jit(solution)/shard_map/pallas_call | solution.py:465
  30.8 1.5 %shard_map.58 = (f32[2,3,3,2,4,256]{5,4,3,2,1,0:T(4,128)}, f32[3,2,3,3,2,4,256]{6,5,4,3,2,1,0:T(4,128)}, f32[2,4]{1,0:T(2,128)}, f32[1,1]{1,0:T(1,128)}) custom-call(f32[2,3,3,2,8,128]{5,4,3,2,1,0:T(8,128)S(1)} %get-tuple-element.12.g_out, f32[3,2,3,3,2,8,128]{6,5,4,3,2,1,0:T(8,128)S(1)} %get-tuple-element.13.v_out, f32[2,4]{1,0:T(2,128)S(1)} %get-tuple-element.14.profile, ...), custom_call_target="tpu_custom_call" | custom-call | tf_op jit(solution)/shard_map/pallas_call | solution.py:493

commit v3 on v2

v3 whole, which is shorter than its diff:
```python
import jax
import jax.numpy as jnp
from jax import lax
from jax.experimental import pallas as pl
from jax.experimental.pallas import tpu as pltpu
from jax.sharding import PartitionSpec as P

ROWS = 8
LANES = 128
Y = 16
PLANES = 4
HALO_ROWS = (3, 7)
EARLY = 4
DEPTH = 8
PLANE = 64
SEMAPHORES = 20
MESH = pl.DeviceIdType.MESH
F32 = jnp.float32


def mul(a, b):
    ar, ai = a
    br, bi = b
    re = im = None
    for k in range(3):
        xr, xi = ar[:, k][:, None], ai[:, k][:, None]
        yr, yi = br[k][None], bi[k][None]
        r = xr * yr - xi * yi
        i = xr * yi + xi * yr
        re, im = (r, i) if re is None else (re + r, im + i)
    return re, im


def mul_dagger(a, b):
    ar, ai = a
    br, bi = b
    re = im = None
    for k in range(3):
        xr, xi = ar[:, k][:, None], ai[:, k][:, None]
        yr, yi = br[:, k][None], bi[:, k][None]
        r = xr * yr + xi * yi
        i = xi * yr - xr * yi
        re, im = (r, i) if re is None else (re + r, im + i)
    return re, im


def dagger_mul(a, b):
    ar, ai = a
    br, bi = b
    re = im = None
    for k in range(3):
        xr, xi = ar[k][:, None], ai[k][:, None]
        yr, yi = br[k][None], bi[k][None]
        r = xr * yr + xi * yi
        i = xr * yi - xi * yr
        re, im = (r, i) if re is None else (re + r, im + i)
    return re, im


def overlap(a, b):
    return jnp.sum(a[0] * b[0] + a[1] * b[1], axis=(0, 1))


def both(fn, pair):
    return fn(pair[0]), fn(pair[1])


def rows_of(shape):
    return lax.broadcasted_iota(jnp.int32, shape, len(shape) - 2)


def lanes_of(shape):
    return lax.broadcasted_iota(jnp.int32, shape, len(shape) - 1)


def pick(mask, a, b):
    return jnp.where(mask, a[0], b[0]), jnp.where(mask, a[1], b[1])


def ahead_x(pair):
    def shift(v):
        near = pltpu.roll(v, LANES - Y, v.ndim - 1)
        far = pltpu.roll(near, PLANES, v.ndim - 2)
        return jnp.where(lanes_of(v.shape) >= LANES - Y, far, near)

    return both(shift, pair)


def ahead_y(pair):
    def shift(v):
        near = pltpu.roll(v, LANES - 1, v.ndim - 1)
        wrap = pltpu.roll(v, Y - 1, v.ndim - 1)
        return jnp.where(lanes_of(v.shape) % Y == Y - 1, wrap, near)

    return both(shift, pair)


def up_z(pair):
    return both(lambda v: pltpu.roll(v, ROWS - 1, v.ndim - 2), pair)


def ahead_z(pair, halo):
    top = rows_of((ROWS, LANES)) % PLANES == PLANES - 1
    return pick(top, halo, up_z(pair))


def or_unit(mask, pair):
    re, im = pair
    return (
        jnp.stack(
            [
                jnp.stack([jnp.where(mask, re[i, j], 1.0 if i == j else 0.0) for j in range(3)])
                for i in range(3)
            ]
        ),
        jnp.where(mask, im, 0.0),
    )


def row_of(ref, row):
    return ref.at[:, :, :, pl.ds(row, 1), :]


def rows_in(ref, count):
    return ref.at[:, :, :, pl.ds(0, count), :]


def drain(ref, sem):
    pltpu.make_async_copy(ref, ref, sem).wait()


def load(ref):
    return ref[0], ref[1]


def kernel(
    time_ref, space_ref, g_out, v_out, small,
    tl, sl, total, scanned, spread, in1, in2, carry, carry_halo, time_halo, space_halo,
    around, part, part_z, part_all, part_back,
    sems, near_sem, far_sem, plane_sem,
):
    (
        load_space, load_time, halo_send, halo_recv, time_send, time_recv,
        send1, recv1, send2, recv2, send3, recv3, send4, recv4,
        send_z, recv_z, send_all, recv_all, send_back, recv_back,
    ) = (sems.at[i] for i in range(SEMAPHORES))
    me = lax.axis_index("ta")
    z = lax.axis_index("gz")
    group, member = me // ROWS, me % ROWS
    below, above = (z + DEPTH - 1) % DEPTH, (z + 1) % DEPTH
    early = z < EARLY

    def in_row(k):
        return group * ROWS + (member + k) % ROWS, z

    def in_column(k):
        return (group + k) % ROWS * ROWS + member, z

    space_loads, time_loads = [], []
    for c in range(2):
        space_loads.append(pltpu.make_async_copy(
            space_ref.at[:, :, :, :, :, :, pl.ds(c * LANES, LANES)],
            sl.at[:, :, :, :, :, pl.ds(c * PLANES, PLANES), :],
            load_space,
        ))
    for c in range(2):
        time_loads.append(pltpu.make_async_copy(
            time_ref.at[:, :, :, :, :, pl.ds(c * LANES, LANES)],
            tl.at[:, :, :, :, pl.ds(c * PLANES, PLANES), :],
            load_time,
        ))
    for copy in space_loads + time_loads:
        copy.start()

    barrier = pltpu.get_barrier_semaphore()

    def greet(device):
        pl.semaphore_signal(barrier, inc=1, device_id=device, device_id_type=MESH)

    greet((me, above))
    for k in range(1, ROWS):
        greet(in_row(k))
    for k in (1, ROWS - 1):
        greet(in_column(k))

    @pl.when(early)
    def _():
        for k in range(2, DEPTH):
            greet((me, (z + k) % DEPTH))

    def time_link(t):
        return tl[0, :, :, t], tl[1, :, :, t]

    def space_link(mu, t):
        return sl[mu, 0, :, :, t], sl[mu, 1, :, :, t]

    def remote(src, dst, send, recv, device):
        return pltpu.make_async_remote_copy(
            src_ref=src, dst_ref=dst, send_sem=send, recv_sem=recv,
            device_id=device, device_id_type=MESH,
        )

    drain(sl, load_space)
    late_below = jnp.logical_or(z == 0, z > EARLY).astype(jnp.int32)
    of_height = jnp.where(early, EARLY - 1, EARLY)
    pl.semaphore_wait(barrier, ROWS - 1 + 2 + of_height + late_below)

    halos = []
    for mu in range(2):
        for c in range(2):
            halos.append(remote(
                sl.at[mu, :, :, :, :, pl.ds(c * PLANES, 1), :],
                space_halo.at[mu, :, :, :, :, pl.ds(HALO_ROWS[c], 1), :],
                halo_send, halo_recv, (me, below),
            ))
    for copy in halos:
        copy.start()

    drain(tl, load_time)
    prod = mul(time_link(0), time_link(1))
    total[0], total[1] = prod

    first = []
    for k in range(1, ROWS):
        first.append(remote(
            row_of(total, (member + k) % ROWS), row_of(in1, member),
            send1, recv1, in_row(k),
        ))
    for copy in first:
        copy.start()
    time_halos = []
    for c in range(2):
        time_halos.append(remote(
            tl.at[:, :, :, 0, pl.ds(c * PLANES, 1), :],
            time_halo.at[:, :, :, pl.ds(HALO_ROWS[c], 1), :],
            time_send, time_recv, (me, below),
        ))
    for copy in time_halos:
        copy.start()

    def tell_rows(sem, distance):
        for k in (distance, ROWS - distance):
            pl.semaphore_signal(sem, inc=1, device_id=in_column(k), device_id_type=MESH)

    tell_rows(near_sem, 1)

    rows = rows_of((ROWS, LANES))
    lanes = lanes_of((ROWS, LANES))
    top = rows % PLANES == PLANES - 1
    traces = []
    for t in range(2):
        ux, uy, uz = (space_link(mu, t) for mu in range(3))
        trace = overlap(mul(ux, ahead_x(uy)), mul(uy, ahead_y(ux)))
        for mu, along, ahead in ((0, ux, ahead_x), (1, uy, ahead_y)):
            rest = dagger_mul(uz, mul(along, ahead(uz)))
            around[mu, 0, :, :, t], around[mu, 1, :, :, t] = rest
            trace = trace + jnp.where(top, 0.0, overlap(rest, up_z(along)))
        traces.append(trace)

    pl.semaphore_wait(near_sem, 2)
    tell_rows(far_sem, 2)

    drain(space_halo.at[:, :, :, :, :, pl.ds(0, 2), :], halo_recv)
    densities = []
    for t in range(2):
        trace = traces[t]
        for mu in range(2):
            rest = around[mu, 0, :, :, t], around[mu, 1, :, :, t]
            beyond = space_halo[mu, 0, :, :, t], space_halo[mu, 1, :, :, t]
            trace = trace + jnp.where(top, overlap(rest, beyond), 0.0)
        densities.append(3.0 - trace * (1.0 / 3.0))

    def spread_sum(v):
        return jnp.broadcast_to(jnp.sum(v, axis=0, keepdims=True), (ROWS, LANES))

    part[0] = spread_sum(densities[0] + densities[1])

    def to_early(height):
        return remote(
            part.at[0, pl.ds(0, 1), :], part_z.at[pl.ds(z, 1), :],
            send_z, recv_z, (me, height),
        )

    for height in range(EARLY):
        @pl.when(z != height)
        def _(height=height):
            to_early(height).start()

    for t in range(2):
        of_row = jnp.sum(densities[t], axis=1, keepdims=True)
        spots = jnp.where(lanes == rows % PLANES, of_row, 0.0)
        profile = jnp.sum(spots, axis=0, keepdims=True) * (1.0 / (3 * 2 * LANES))
        small[t : t + 1, :] = profile

    drain(rows_in(in1, ROWS - 1), recv1)
    scan = pick(rows == member, load(total), load(in1))
    for s in (1, 2, 4):
        earlier = both(lambda v: pltpu.roll(v, s, 2), scan)
        scan = pick(rows >= s, mul(earlier, scan), scan)
    scanned[0], scanned[1] = scan

    def to_later(k):
        return remote(
            row_of(scanned, ROWS - 1), row_of(in2, group),
            send2, recv2, in_column(k),
        )

    pl.semaphore_wait(far_sem, 2)

    @pl.when(early)
    def _():
        for k in range(1, ROWS):
            pl.semaphore_signal(plane_sem, inc=1, device_id=in_row(k), device_id_type=MESH)

    for k in range(ROWS - 1, 0, -1):
        @pl.when(group + k < ROWS)
        def _(k=k):
            to_later(k).start()

    inside = or_unit(rows >= 1, both(lambda v: pltpu.roll(v, 1, 2), scan))
    for k in range(1, ROWS):
        @pl.when(group == k)
        def _(k=k):
            drain(rows_in(in2, k), recv2)
    before = or_unit(rows < group, load(in2))
    for s in (1, 2, 4):
        before = mul(before, both(lambda v: pltpu.roll(v, ROWS - s, 2), before))
    before = both(lambda v: jnp.broadcast_to(v[:, :, 0:1], v.shape), before)
    spread[0], spread[1] = mul(before, inside)

    def return_carries():
        for k in range(1, ROWS):
            remote(
                row_of(spread, (member + k) % ROWS), row_of(carry, member),
                send3, recv3, in_row(k),
            ).start()

    ahead = group < ROWS // 2

    @pl.when(ahead)
    def _():
        return_carries()

    def to_plane(row, k):
        return remote(
            part.at[1, pl.ds(0, 1), :], part_all.at[group, pl.ds(member, 1), :],
            send_all, recv_all, (row * ROWS + (member + k) % ROWS, z),
        )

    @pl.when(early)
    def _():
        drain(part_z.at[pl.ds(0, DEPTH - 1), :], recv_z)
        part[1] = spread_sum(jnp.where(rows == z, part[0], part_z[...]))
        pl.semaphore_wait(plane_sem, ROWS - 1)
        for row in range(ROWS):
            @pl.when(row != group)
            def _(row=row):
                to_plane(row, 0).start()

            for k in range(1, ROWS):
                to_plane(row, k).start()

    @pl.when(jnp.logical_not(ahead))
    def _():
        return_carries()

    drain(rows_in(carry, ROWS - 1), recv3)
    g0 = pick(rows == member, load(spread), load(carry))
    g1 = mul(g0, time_link(0))
    g = (g0, g1)
    for t in range(2):
        g_out[0, :, :, t], g_out[1, :, :, t] = g[t]
    for c in range(2):
        remote(
            g_out.at[:, :, :, 0, pl.ds(c * PLANES, 1), :],
            carry_halo.at[:, :, :, pl.ds(HALO_ROWS[c], 1), :],
            send4, recv4, (me, below),
        ).start()

    def fix(mu, t, ahead):
        v = mul_dagger(mul(g[t], space_link(mu, t)), ahead)
        v_out[mu, 0, :, :, t], v_out[mu, 1, :, :, t] = v

    for t in range(2):
        fix(0, t, ahead_x(g[t]))
    for t in range(2):
        fix(1, t, ahead_y(g[t]))
    drain(rows_in(time_halo, 2), time_recv)
    drain(rows_in(carry_halo, 2), recv4)
    g0z = ahead_z(g0, load(carry_halo))
    g1z = mul(g0z, ahead_z(time_link(0), load(time_halo)))
    for t, ahead in ((0, g0z), (1, g1z)):
        fix(2, t, ahead)

    plane_rows = in1.at[pl.ds(0, 1), :, :, pl.ds(0, ROWS - 1), :]

    def to_late(height):
        return remote(part.at[2], part_back, send_back, recv_back, (me, height))

    def tell_late(act):
        @pl.when(z == EARLY - 1)
        def _():
            for height in range(EARLY, DEPTH - 1):
                act(to_late(height))

        @pl.when(z == EARLY - 2)
        def _():
            act(to_late(DEPTH - 1))

    def write_mean(sites):
        mean = jnp.sum(sites[0:1], axis=1, keepdims=True)
        small[2:3, :] = jnp.broadcast_to(mean * (1.0 / (3 * 2 * LANES * 4096)), (1, LANES))

    @pl.when(early)
    def _():
        drain(plane_rows, recv_all)
        parts = None
        for k in range(ROWS):
            mine = jnp.logical_and(rows == member, group == k)
            got = jnp.where(mine, part[1], part_all[k])
            parts = got if parts is None else parts + got
        whole = spread_sum(parts)
        part[2] = whole
        tell_late(lambda copy: copy.start())
        write_mean(whole)
        drain(plane_rows, send_all)
        drain(part.at[0, pl.ds(0, EARLY - 1), :], send_z)

    @pl.when(jnp.logical_not(early))
    def _():
        drain(part_back, recv_back)
        write_mean(part_back[...])
        drain(part.at[0, pl.ds(0, EARLY), :], send_z)

    drain(space_halo.at[:, :, :, :, :, pl.ds(0, 2), :], halo_send)
    drain(rows_in(time_halo, 2), time_send)
    drain(rows_in(in1, ROWS - 1), send1)
    drain(rows_in(carry, ROWS - 1), send3)
    for k in range(1, ROWS):
        @pl.when(group == ROWS - 1 - k)
        def _(k=k):
            drain(rows_in(in2, k), send2)

    drain(rows_in(carry_halo, 2), send4)

    @pl.when(z == EARLY - 1)
    def _():
        drain(part, send_back)

    @pl.when(z == EARLY - 2)
    def _():
        drain(part_back, send_back)


def write_out(
    g_out, v_out, small, gauge_ref, fixed_ref, profile_ref, mean_ref, profile, mean, sem
):
    profile[...] = small[0:2, :PLANES]
    mean[...] = small[2:3, 0:1]
    copies = []
    for c in range(2):
        planes, lanes = pl.ds(c * PLANES, PLANES), pl.ds(c * LANES, LANES)
        for src, dst in (
            (v_out.at[:, :, :, :, :, planes, :], fixed_ref.at[:, :, :, :, :, :, lanes]),
            (g_out.at[:, :, :, :, planes, :], gauge_ref.at[:, :, :, :, :, lanes]),
        ):
            copies.append(pltpu.make_async_copy(src, dst, sem.at[len(copies)]))
    for src, dst in ((profile, profile_ref), (mean, mean_ref)):
        copies.append(pltpu.make_async_copy(src, dst, sem.at[len(copies)]))
    for copy in copies:
        copy.start()
    for copy in copies:
        copy.wait()


def on_device(time_links, space_links):
    pair = (2, 3, 3, ROWS, LANES)
    vmem = pl.BlockSpec(memory_space=pltpu.VMEM)
    anywhere = pl.BlockSpec(memory_space=pl.ANY)
    staged = pl.pallas_call(
        kernel,
        out_shape=(
            pltpu.VMEM((2, 3, 3, 2, ROWS, LANES), F32),
            pltpu.VMEM((3, 2, 3, 3, 2, ROWS, LANES), F32),
            pltpu.VMEM((ROWS, LANES), F32),
        ),
        in_specs=[pl.BlockSpec(memory_space=pltpu.HBM)] * 2,
        out_specs=(vmem,) * 3,
        scratch_shapes=[
            pltpu.VMEM((2, 3, 3, 2, ROWS, LANES), F32),
            pltpu.VMEM((3, 2, 3, 3, 2, ROWS, LANES), F32),
            *[pltpu.VMEM(pair, F32)] * 8,
            pltpu.VMEM((2, 2, 3, 3, 2, ROWS, LANES), F32),
            pltpu.VMEM((2, 2, 3, 3, 2, ROWS, LANES), F32),
            pltpu.VMEM((3, ROWS, LANES), F32),
            pltpu.VMEM((ROWS, LANES), F32),
            pltpu.VMEM((ROWS, ROWS, LANES), F32),
            pltpu.VMEM((ROWS, LANES), F32),
            pltpu.SemaphoreType.DMA((SEMAPHORES,)),
            *[pltpu.SemaphoreType.REGULAR] * 3,
        ],
        compiler_params=pltpu.CompilerParams(collective_id=0, has_side_effects=True),
    )(time_links, space_links)
    gauge, fixed, profile, mean = pl.pallas_call(
        write_out,
        out_shape=(
            jax.ShapeDtypeStruct(time_links.shape, F32),
            jax.ShapeDtypeStruct(space_links.shape, F32),
            jax.ShapeDtypeStruct((2, PLANES), F32),
            jax.ShapeDtypeStruct((1, 1), F32),
        ),
        in_specs=[vmem] * 3,
        out_specs=(anywhere,) * 4,
        scratch_shapes=[
            pltpu.VMEM((2, PLANES), F32), pltpu.VMEM((1, 1), F32), pltpu.SemaphoreType.DMA((6,)),
        ],
        compiler_params=pltpu.CompilerParams(vmem_limit_bytes=4 * 2**20),
    )(*staged)
    return gauge, fixed, profile, mean.reshape(())


def solution(mesh):
    placed = (P(None, None, None, "ta", "gz", None), P(None, None, None, None, "ta", "gz", None))
    return jax.shard_map(
        on_device,
        mesh=mesh,
        in_specs=placed,
        out_specs=(*placed, P("ta", "gz"), P()),
        check_vma=False,
    )
```

time: 32.4 us -> 30.2 us (0.932)
  Pallas kernels: 31.7 us -> 29.4 us
    pallas_call x1, Pallas kernels: 30.2 us -> 28.5 us  [on_device(): pl.pallas_call(kernel, out_shape=(pltpu.VMEM((2, 3, 3, 2, ROWS, LANES), F...]
    pallas_call x1, Pallas kernels: 1.49 us -> 0.86 us  [on_device(): pl.pallas_call(write_out, out_shape=(jax.ShapeDtypeStruct(time_links.shap...]
where the time goes in v3:
time: 30.2 us; the launch traced here: 30 us
  Pallas kernels  29.4 us (97%)
  between operations  0.64 us (2%)
    pallas_call x1, Pallas kernels, on_device(): pl.pallas_call(kernel, out_shape=(pltpu.VMEM((2, 3, 3, 2, ROWS, LANES), F...  28.5 us
    pallas_call x1, Pallas kernels, on_device(): pl.pallas_call(write_out, out_shape=(jax.ShapeDtypeStruct(time_links.shap...  0.86 us

profile of v3, /device:TPU:1, one launch (start us, length us, event | category | flops | bytes accessed | tf_op | source)
XLA Modules:
  0.0 30.0 jit_solution(7646051215966942042)
XLA Ops:
  0.6 28.5 %shard_map.57 = (f32[2,3,3,2,8,128]{5,4,3,2,1,0:T(8,128)S(1)}, f32[3,2,3,3,2,8,128]{6,5,4,3,2,1,0:T(8,128)S(1)}, f32[8,128]{1,0:T(8,128)S(1)}) custom-call(f32[2,3,3,2,4,256]{5,4,3,2,1,0:T(4,128)} %time_ref.1, f32[3,2,3,3,2,4,256]{6,5,4,3,2,1,0:T(4,128)} %space_ref.1), custom_call_target="tpu_custom_call" | custom-call | tf_op jit(solution)/shard_map/pallas_call | solution.py:480
  29.2 0.9 %shard_map.58 = (f32[2,3,3,2,4,256]{5,4,3,2,1,0:T(4,128)}, f32[3,2,3,3,2,4,256]{6,5,4,3,2,1,0:T(4,128)}, f32[2,4]{1,0:T(2,128)}, f32[1,1]{1,0:T(1,128)}) custom-call(f32[2,3,3,2,8,128]{5,4,3,2,1,0:T(8,128)S(1)} %get-tuple-element.11.g_out, f32[3,2,3,3,2,8,128]{6,5,4,3,2,1,0:T(8,128)S(1)} %get-tuple-element.12.v_out, f32[8,128]{1,0:T(8,128)S(1)} %get-tuple-element.13.small), custom_call_target="tpu_custom_call" | custom-call | tf_op jit(solution)/shard_map/pallas_call | solution.py:504
